TPU v7x, 32 devices: a whole 2x2x4 slice. The times are simulated.
32 devices in a mesh: clips: 1, frame: 32 (over z, y, x, core).
Axes of the slice: x: 2, y: 2, z: 4, core: 2. Of those that a mesh axis runs over, the one named last changes fastest.
Arguments:
- frame_sequence_elements: bfloat16 [32, 256, 1280], P(('clips', 'frame')), may hold values from -8 to 8
- entry_rescaling_factors: float32 [1280], replicated, may hold values from 0.5 to 1.5
- asking_projection_tensor: bfloat16 [1280, 640], replicated, may hold values from -1 to 1
- lookup_projection_tensor: bfloat16 [1280, 640], replicated, may hold values from -1 to 1
- content_projection_tensor: bfloat16 [1280, 640], replicated, may hold values from -0.15625 to 0.15625
- logit_sharpness: float32 [5], replicated, may hold values from 0.3 to 24
- final_projection_tensor: bfloat16 [640, 1280], replicated, may hold values from -0.25 to 0.25
Outputs:
- mixed: bfloat16 [32, 256, 1280], P(('clips', 'frame'))
All inputs are finite; a program needn't handle non-finite values.
Results may differ from a plain program's by a relative error of at most 0.006.
Values may be sent and summed in bfloat16 or wider, within the bound.
A program may use at most 64 MiB of HBM per device.

v0:
```python
import math

import jax
import jax.numpy as jnp
from jax import lax
from jax.sharding import PartitionSpec as P

HEADS_WIN = 5
CHANNELS_PER_ATT = 128
WINDOW = 32


epsilon = 1e-06


def quadratic_average_rescaling(values):
    return values * lax.rsqrt(jnp.mean(values * values, axis=-1, keepdims=True) + epsilon)


def project_through(
    incoming_token_vectors,
    asking_projection_tensor,
    lookup_projection_tensor,
    content_projection_tensor,
    logit_sharpness,
):
    lead = incoming_token_vectors.shape[:-1]
    flat_rows = incoming_token_vectors.reshape(-1, incoming_token_vectors.shape[-1])
    shape_heads = lead + (HEADS_WIN, CHANNELS_PER_ATT)
    asking_vectors_full = jnp.dot(
        flat_rows, asking_projection_tensor, preferred_element_type=jnp.float32
    ).reshape(shape_heads)
    k_full = jnp.dot(
        flat_rows, lookup_projection_tensor, preferred_element_type=jnp.float32
    ).reshape(shape_heads)
    v_full = jnp.dot(
        flat_rows, content_projection_tensor, preferred_element_type=jnp.float32
    ).reshape(shape_heads)
    asking_token_vectors = (
        quadratic_average_rescaling(asking_vectors_full)
        * logit_sharpness[:, None]
        / math.sqrt(CHANNELS_PER_ATT)
    ).astype(jnp.bfloat16)
    key_matrix_rows = quadratic_average_rescaling(k_full).astype(jnp.bfloat16)
    return (asking_token_vectors, key_matrix_rows, v_full.astype(jnp.bfloat16))


def softmax_bf16(scores, window_mask):
    scores = jnp.where(window_mask, scores, -1e30)
    top = jnp.max(scores, axis=-1, keepdims=True)
    expo = jnp.exp(scores - top)
    return (expo / jnp.sum(expo, axis=-1, keepdims=True)).astype(jnp.bfloat16)


def band_attention(asking_token_vectors, key_matrix_rows, value_matrix_rows):
    all_frames, positions, heads, width = asking_token_vectors.shape
    blocks = all_frames // WINDOW
    block_shape = (blocks, WINDOW, positions, heads, width)
    q_blocks = asking_token_vectors.reshape(block_shape)
    k_blocks = key_matrix_rows.reshape(block_shape)
    v_blocks = value_matrix_rows.reshape(block_shape)
    k_earlier = jnp.concatenate([jnp.zeros_like(k_blocks[:1]), k_blocks[:-1]], axis=0)
    v_earlier = jnp.concatenate([jnp.zeros_like(v_blocks[:1]), v_blocks[:-1]], axis=0)
    k_pair = jnp.concatenate([k_earlier, k_blocks], axis=1)
    v_pair = jnp.concatenate([v_earlier, v_blocks], axis=1)
    scores = jnp.einsum("bqphd,bkphd->bphqk", q_blocks, k_pair, preferred_element_type=jnp.float32)
    block_ids = jnp.arange(blocks, dtype=jnp.int32)[:, None, None]
    row_ids = jnp.arange(WINDOW, dtype=jnp.int32)[None, :, None]
    col_ids = jnp.arange(2 * WINDOW, dtype=jnp.int32)[None, None, :]
    offset = row_ids - col_ids + WINDOW
    inside = (offset >= 0) & (offset < WINDOW) & (block_ids * WINDOW - WINDOW + col_ids >= 0)
    weights = softmax_bf16(scores, inside[:, None, None])
    attended = jnp.einsum("bphqk,bkphd->bqphd", weights, v_pair, preferred_element_type=jnp.float32)
    return attended.astype(jnp.bfloat16).reshape(all_frames, positions, heads, width)


def local(
    frame_sequence_elements,
    entry_rescaling_factors,
    asking_projection_tensor,
    lookup_projection_tensor,
    content_projection_tensor,
    logit_sharpness,
    final_projection_tensor,
):
    frames_dev, seq_len, width = frame_sequence_elements.shape
    floated = frame_sequence_elements.astype(jnp.float32)
    rescaled_token_vectors = (
        quadratic_average_rescaling(floated) * entry_rescaling_factors
    ).astype(jnp.bfloat16)
    position_rows = lax.all_to_all(
        rescaled_token_vectors, "frame", split_axis=1, concat_axis=0, tiled=True
    )
    asking_token_vectors, key_matrix_rows, value_matrix_rows = project_through(
        position_rows,
        asking_projection_tensor,
        lookup_projection_tensor,
        content_projection_tensor,
        logit_sharpness,
    )
    result = band_attention(asking_token_vectors, key_matrix_rows, value_matrix_rows)
    attended = lax.all_to_all(result, "frame", split_axis=0, concat_axis=1, tiled=True)
    flat_attended = attended.reshape(frames_dev * seq_len, -1)
    summed = jnp.dot(
        flat_attended, final_projection_tensor, preferred_element_type=jnp.float32
    ) + floated.reshape(frames_dev * seq_len, width)
    return summed.astype(jnp.bfloat16).reshape(frames_dev, seq_len, width)


def solution(mesh):
    placed = (P(("clips", "frame"), None, None), P(), P(), P(), P(), P(), P())
    return jax.shard_map(
        local,
        mesh=mesh,
        in_specs=placed,
        out_specs=P(("clips", "frame"), None, None),
        check_vma=False,
    )
```

profile of v0, /device:TPU:0, one launch (start us, length us, event | category | flops | bytes accessed | tf_op | source)
XLA Modules:
  0.0 71.8 jit_solution(14591210048889410213)
XLA Ops:
  0.0 0.0 copy-start
  0.0 1.4 %fusion.4 = f32[256]{0:T(256)S(1)} fusion(bf16[1,256,1280]{2,1,0:T(8,128)(2,1)} %param.7), kind=kLoop, calls=%fused_computation.8 | loop fusion | flops 982784 | bytes 656384 | tf_op jit(solution)/shard_map/reduce_sum | solution.py:17
  1.4 1.3 %fusion.6 = bf16[1,256,1280]{2,1,0:T(8,128)(2,1)S(1)} fusion(bf16[1,256,1280]{2,1,0:T(8,128)(2,1)} %param.7, f32[1280]{0:T(1024)} %param.8, f32[256]{0:T(256)S(1)} %add_rsqrt_fusion.2), kind=kLoop, calls=%fused_computation.10 | loop fusion | flops 1310720 | bytes 1316864 | tf_op jit(solution)/shard_map/convert_element_type | solution.py:90
  2.7 1.0 %copy.92 = bf16[1,256,1280]{2,0,1:T(2,128)(2,1)S(1)} copy(bf16[1,256,1280]{2,1,0:T(8,128)(2,1)S(1)} %fusion.6) | data formatting | bytes 1310720 | tf_op jit(solution)/shard_map/convert_element_type | solution.py:90
  3.8 0.6 broadcast.125
  4.4 5.5 %reduce.5 = bf16[256,1280]{1,0:T(8,128)(2,1)} reduce(bf16[256,1,1280]{2,1,0:T(2,128)(2,1)S(1)} %bitcast.61, bf16[]{:T(256)} %broadcast.125), dimensions={1}, to_apply=%bitcast.60.reduce_sub_computation | reduce | bytes 1310722
  9.9 2.7 %reshape.174 = bf16[32,2,5120]{2,1,0:T(2,128)(2,1)} reshape(bf16[256,1280]{1,0:T(8,128)(2,1)} %reduce.5) | data formatting | bytes 1310720
  12.5 7.5 %all-to-all-start = ((bf16[32,2,5120]{2,1,0:T(2,128)(2,1)}), bf16[32,2,5120]{2,1,0:T(2,128)(2,1)S(1)}, u32[]{:S(2)}, u32[]{:S(2)}) async-start(bf16[32,2,5120]{2,1,0:T(2,128)(2,1)} %reshape.174), calls=%async_computation | async-start | bytes 1310720 | tf_op jit(solution)/shard_map/all_to_all | solution.py:91
  20.0 3.6 %copy.57 = bf16[1280,640]{0,1:T(8,128)(2,1)} copy(bf16[1280,640]{1,0:T(8,128)(2,1)} %param.9) | data formatting | bytes 3276800 | tf_op args[2]
  23.6 3.5 %copy.60 = bf16[1280,640]{0,1:T(8,128)(2,1)} copy(bf16[1280,640]{1,0:T(8,128)(2,1)} %param.10) | data formatting | bytes 3276800 | tf_op args[3]
  27.1 3.6 %copy.56 = bf16[1280,640]{0,1:T(8,128)(2,1)} copy(bf16[1280,640]{1,0:T(8,128)(2,1)} %param.11) | data formatting | bytes 3276800 | tf_op args[4]
  30.7 7.1 %all-to-all-done = bf16[32,2,5120]{2,1,0:T(2,128)(2,1)S(1)} async-done(((bf16[32,2,5120]{2,1,0:T(2,128)(2,1)}), bf16[32,2,5120]{2,1,0:T(2,128)(2,1)S(1)}, u32[]{:S(2)}, u32[]{:S(2)}) %all-to-all-start) | async-done | bytes 655392 | tf_op jit(solution)/shard_map/all_to_all | solution.py:91
  37.8 1.8 %reshape.175 = bf16[256,1,1280]{2,1,0:T(2,128)(2,1)} reshape(bf16[32,2,5120]{2,1,0:T(2,128)(2,1)S(1)} %all-to-all-done) | data formatting | bytes 1310720
  39.7 3.5 %multiply_reduce_fusion.1 = (f32[32,8,5]{1,2,0:T(8,128)S(1)}, f32[32,8,5,128]{3,1,2,0:T(8,128)}) fusion(bf16[5,128,1280,1]{2,1,0,3:T(8,128)(2,1)} %bitcast.64, bf16[1,256,1280]{2,0,1:T(2,128)(2,1)} %bitcast.65), kind=kOutput, calls=%fused_computation.29 | convolution fusion | flops 419756800 | bytes 2954240 | tf_op jit(solution)/shard_map/dot_general | solution.py:30
  43.2 0.1 copy.58
  43.3 0.1 copy.59
  43.4 2.9 %multiply_reduce_fusion = (f32[32,8,5]{1,2,0:T(8,128)S(1)}, f32[32,8,5,128]{3,1,2,0:T(8,128)}) fusion(bf16[5,128,1280,1]{2,1,0,3:T(8,128)(2,1)S(1)} %bitcast.63, bf16[1,256,1280]{2,0,1:T(2,128)(2,1)} %bitcast.66), kind=kOutput, calls=%fused_computation.27 | convolution fusion | flops 419756800 | bytes 2954240 | tf_op jit(solution)/shard_map/dot_general | solution.py:33
  46.3 0.1 copy.61
  46.4 0.1 copy.62
  46.6 1.3 %fusion.17 = bf16[1,32,8,5,128]{4,2,3,1,0:T(8,128)(2,1)S(1)} fusion(f32[32,8,5,128]{3,1,2,0:T(8,128)} %get-tuple-element.6, f32[32,8,5]{1,2,0:T(8,128)S(1)} %copy.62), kind=kLoop, calls=%fused_computation.31 | loop fusion | flops 327680 | bytes 988160 | tf_op jit(solution)/shard_map/reshape | solution.py:60
  47.9 0.1 pad_bitcast_fusion
  48.0 0.3 multiply_convert_fusion.1
  48.3 0.5 convolution_select_fusion
  48.7 0.4 fusion.29
  49.2 0.3 copy-done.2
  49.4 0.4 copy-done.4
  49.8 0.7 %fusion.9 = bf16[1,32,8,5,128]{4,2,3,1,0:T(8,128)(2,1)S(1)} fusion(bf16[5,128,1280,1]{2,1,0,3:T(8,128)(2,1)S(1)} %bitcast.62, bf16[1,256,1280]{2,0,1:T(2,128)(2,1)S(1)} %bitcast.67), kind=kOutput, calls=%fused_computation.16 | convolution fusion | flops 419594240 | bytes 2621440 | tf_op jit(solution)/shard_map/dot_general | solution.py:36
  50.5 0.9 %pad_bitcast_fusion.1 = bf16[64,8,5,128]{3,1,2,0:T(8,128)(2,1)} fusion(bf16[1,32,8,5,128]{4,2,3,1,0:T(8,128)(2,1)S(1)} %fusion.9), kind=kLoop, calls=%fused_computation.30 | loop fusion | bytes 983040 | tf_op jit(solution)/shard_map/reshape.26
  51.4 3.4 %fusion.8 = bf16[32,8,5,128]{3,0,2,1:T(8,128)(2,1)S(1)} fusion(bf16[64,8,5,128]{3,1,2,0:T(8,128)(2,1)} %pad_bitcast_fusion.1, f32[8,5,32]{2,1,0:T(8,128)S(1)} %fusion.29, f32[8,5,32,64]{3,2,1,0:T(8,128)S(1)} %convolution_select_fusion), kind=kOutput, calls=%fused_computation.15 | convolution fusion | flops 21382464 | bytes 1315840 | tf_op jit(solution)/shard_map/bphqk,bkphd->bqphd/dot_general | solution.py:73
  54.9 0.1 copy.66
  55.0 15.3 %all_to_all.8 = bf16[32,8,5,128]{3,1,2,0:T(8,128)(2,1)S(1)} all-to-all(bf16[32,8,5,128]{3,1,2,0:T(8,128)(2,1)S(1)} %copy.66), channel_id=1, replica_groups=mesh['clips'=1,'frame'=32] {'frame'}, dimensions={0} | all-to-all | bytes 655360 | tf_op jit(solution)/shard_map/all_to_all | solution.py:102
  70.3 1.5 %fusion.2 = bf16[1,256,1280]{2,1,0:T(8,128)(2,1)} fusion(bf16[640,1280]{1,0:T(8,128)(2,1)S(1)} %copy-done, bf16[1,256,1280]{2,1,0:T(8,128)(2,1)S(1)} %copy-done.1, bf16[32,8,5,128]{3,1,2,0:T(8,128)(2,1)S(1)} %all_to_all.8), kind=kOutput, calls=%fused_computation.3 | convolution fusion | flops 420413440 | bytes 3276800 | tf_op jit(solution)/shard_map/dot_general | solution.py:104
  (16 shorter events, 0.1 us)
Async XLA Ops:
  0.0 70.3 %copy-start = (bf16[640,1280]{1,0:T(8,128)(2,1)S(1)}, bf16[640,1280]{1,0:T(8,128)(2,1)}, u32[]{:S(2)}) copy-start(bf16[640,1280]{1,0:T(8,128)(2,1)} %param.13) | copy-start | bytes 4915204
  12.5 25.3 %all-to-all-start = ((bf16[32,2,5120]{2,1,0:T(2,128)(2,1)}), bf16[32,2,5120]{2,1,0:T(2,128)(2,1)S(1)}, u32[]{:S(2)}, u32[]{:S(2)}) async-start(bf16[32,2,5120]{2,1,0:T(2,128)(2,1)} %reshape.174), calls=%async_computation | async-start | bytes 1310720 | tf_op jit(solution)/shard_map/all_to_all | solution.py:91
  39.7 3.7 %copy-start.3 = (bf16[1280,640]{0,1:T(8,128)(2,1)S(1)}, bf16[1280,640]{0,1:T(8,128)(2,1)}, u32[]{:S(2)}) copy-start(bf16[1280,640]{0,1:T(8,128)(2,1)} %copy.60) | copy-start | bytes 4915204
  46.3 1.6 %copy-start.5 = (f32[32,8,5,128]{3,1,2,0:T(8,128)S(1)}, f32[32,8,5,128]{3,1,2,0:T(8,128)}, u32[]{:S(2)}) copy-start(f32[32,8,5,128]{3,1,2,0:T(8,128)} %get-tuple-element.8) | copy-start | bytes 1966084
  46.3 1.6 %copy-start.6 = (f32[5]{0:T(128)S(1)}, f32[5]{0:T(128)}, u32[]{:S(2)}) copy-start(f32[5]{0:T(128)} %param.12) | copy-start | bytes 64
  48.0 1.4 %copy-start.2 = (bf16[1280,640]{0,1:T(8,128)(2,1)S(1)}, bf16[1280,640]{0,1:T(8,128)(2,1)}, u32[]{:S(2)}) copy-start(bf16[1280,640]{0,1:T(8,128)(2,1)} %copy.56) | copy-start | bytes 4915204
  48.0 1.8 %copy-start.4 = (bf16[256,1,1280]{2,1,0:T(2,128)(2,1)S(1)}, bf16[256,1,1280]{2,1,0:T(2,128)(2,1)}, u32[]{:S(2)}) copy-start(bf16[256,1,1280]{2,1,0:T(2,128)(2,1)} %reshape.175) | copy-start | bytes 1966084
  51.4 18.8 %copy-start.1 = (bf16[1,256,1280]{2,1,0:T(8,128)(2,1)S(1)}, bf16[1,256,1280]{2,1,0:T(8,128)(2,1)}, u32[]{:S(2)}) copy-start(bf16[1,256,1280]{2,1,0:T(8,128)(2,1)} %param.7) | copy-start | bytes 1966084
where the time goes:
time: 72.4 us; the launch traced here: 71.8 us
  local copies, waits for them, and re-layouts  19 us (26%)
  blocking collectives  15.3 us (21%)
  matrix products  12.5 us (17%)
  other arithmetic  10.3 us (14%)
  starting transfers between devices  7.51 us (10%)
  waiting for transfers between devices  7.12 us (10%)
    unnamed x20, local copies, waits for them, and re-layouts  16.4 us
    all_to_all x1, blocking collectives, local(): lax.all_to_all(result, 'frame', split_axis=0, concat_axis=1, tiled=True)  15.3 us
    all_to_all x1, starting transfers between devices, local(): lax.all_to_all(rescaled_token_vectors, 'frame', split_axis=1, concat_axis...  7.51 us
    all_to_all x1, waiting for transfers between devices, local(): lax.all_to_all(rescaled_token_vectors, 'frame', split_axis=1, concat_axis...  7.12 us
    unnamed x1, other arithmetic  5.49 us
    dot_general x1, matrix products, project_through(): jnp.dot(flat_rows, asking_projection_tensor, preferred_element_type=jnp.f...  3.52 us
    dot_general x1, matrix products, band_attention(): jnp.einsum('bphqk,bkphd->bqphd', weights, v_pair, preferred_element_type=...  3.44 us
    dot_general x1, matrix products, project_through(): jnp.dot(flat_rows, lookup_projection_tensor, preferred_element_type=jnp.f...  2.88 us
  transfers between devices with their start and end apart: 1, of which 1 were waited for; matrix products, arithmetic and copies ran while one was open for 15% of the time, Pallas kernels for 0%

commit v1 on v0

--- a/solution.py
+++ b/solution.py
@@ -1,8 +1,11 @@
+import functools
 import math
 
 import jax
 import jax.numpy as jnp
 from jax import lax
+from jax.experimental import pallas as pl
+from jax.experimental.pallas import tpu as pltpu
 from jax.sharding import PartitionSpec as P
 
 HEADS_WIN = 5
@@ -107,10 +110,208 @@
     return summed.astype(jnp.bfloat16).reshape(frames_dev, seq_len, width)
 
 
+MESH = pl.DeviceIdType.MESH
+HIGH = HEADS_WIN * CHANNELS_PER_ATT
+
+
+def visiting_order(devices):
+    return sorted(range(1, devices), key=lambda k: (abs(k - devices // 2), k))
+
+
+def fused(
+    devices,
+    local_frames,
+    sharp_ref,
+    x_hbm,
+    gain_ref,
+    wq_hbm,
+    wk_hbm,
+    wv_hbm,
+    wo_hbm,
+    out_ref,
+    x_own,
+    wq,
+    wk,
+    wv,
+    wo,
+    gathered,
+    q_rows,
+    k_rows,
+    v_rows,
+    outgoing,
+    returned,
+    load_sem,
+    send_a,
+    recv_a,
+    send_b,
+    recv_b,
+):
+    me = lax.axis_index("frame")
+    block, width = x_own.shape[1], x_own.shape[2]
+    positions = block // local_frames
+    order = visiting_order(devices)
+
+    barrier = pltpu.get_barrier_semaphore()
+    for k in order:
+        pl.semaphore_signal(
+            barrier, inc=1, device_id={"frame": lax.rem(me + k, devices)}, device_id_type=MESH
+        )
+    loads = [
+        pltpu.make_async_copy(source, target, load_sem.at[i])
+        for i, (source, target) in enumerate(
+            ((x_hbm, x_own), (wq_hbm, wq), (wk_hbm, wk), (wv_hbm, wv), (wo_hbm, wo))
+        )
+    ]
+    for load in loads:
+        load.start()
+    loads[0].wait()
+    pl.semaphore_wait(barrier, devices - 1)
+
+    first = {}
+    for k in order:
+        target = lax.rem(me + k, devices)
+        first[k] = pltpu.make_async_remote_copy(
+            src_ref=x_own.at[target],
+            dst_ref=gathered.at[k],
+            send_sem=send_a.at[k],
+            recv_sem=recv_a.at[k],
+            device_id={"frame": target},
+            device_id_type=MESH,
+        )
+        first[k].start()
+    gathered[0] = x_own[me]
+    for load in loads[1:]:
+        load.wait()
+
+    def project(start, stop):
+        rows = (stop - start) * block
+        at = slice(start * block, stop * block)
+        x = gathered[start:stop].astype(jnp.float32).reshape(rows, width)
+        normed = (quadratic_average_rescaling(x) * gain_ref[...]).astype(jnp.bfloat16)
+        q = jnp.dot(normed, wq[...], preferred_element_type=jnp.float32)
+        k = jnp.dot(normed, wk[...], preferred_element_type=jnp.float32)
+        v = jnp.dot(normed, wv[...], preferred_element_type=jnp.float32)
+        for h in range(HEADS_WIN):
+            c = slice(h * CHANNELS_PER_ATT, (h + 1) * CHANNELS_PER_ATT)
+            q_rows[at, c] = (
+                quadratic_average_rescaling(q[:, c]) * sharp_ref[h] / math.sqrt(CHANNELS_PER_ATT)
+            ).astype(jnp.bfloat16)
+            k_rows[at, c] = quadratic_average_rescaling(k[:, c]).astype(jnp.bfloat16)
+        v_rows[at, :] = v.astype(jnp.bfloat16)
+
+    quarter = devices // 4
+    pieces = ((quarter, devices - quarter), (devices - quarter, devices), (0, quarter))
+    for start, stop in pieces:
+        for k in range(max(start, 1), stop):
+            first[k].wait_recv()
+        project(start, stop)
+
+    total = devices * block
+    def ids(axis):
+        r = lax.broadcasted_iota(jnp.int32, (total, total), axis)
+        slot = r // block
+        owner = me - slot
+        owner = jnp.where(owner < 0, owner + devices, owner)
+        inner = r - slot * block
+        return owner * local_frames + inner // positions, inner % positions
+
+    t_row, p_row = ids(0)
+    t_col, p_col = ids(1)
+    offset = t_row - t_col
+    inside = (p_row == p_col) & (offset >= 0) & (offset < WINDOW)
+    for h in range(HEADS_WIN):
+        c = slice(h * CHANNELS_PER_ATT, (h + 1) * CHANNELS_PER_ATT)
+        scores = lax.dot_general(
+            q_rows[:, c], k_rows[:, c], (((1,), (1,)), ((), ())), preferred_element_type=jnp.float32
+        )
+        weights = softmax_bf16(scores, inside)
+        attended = jnp.dot(weights, v_rows[:, c], preferred_element_type=jnp.float32)
+        outgoing[:, :, c] = attended.reshape(devices, block, CHANNELS_PER_ATT).astype(jnp.bfloat16)
+
+    second = {}
+    for k in order:
+        target = lax.rem(me + devices - k, devices)
+        second[k] = pltpu.make_async_remote_copy(
+            src_ref=outgoing.at[k],
+            dst_ref=returned.at[me],
+            send_sem=send_b.at[k],
+            recv_sem=recv_b.at[k],
+            device_id={"frame": target},
+            device_id_type=MESH,
+        )
+        second[k].start()
+    returned[me] = outgoing[0]
+    for k in order:
+        pltpu.make_async_remote_copy(
+            src_ref=outgoing.at[k],
+            dst_ref=returned.at[lax.rem(me + k, devices)],
+            send_sem=send_b.at[k],
+            recv_sem=recv_b.at[k],
+            device_id={"frame": lax.rem(me + devices - k, devices)},
+            device_id_type=MESH,
+        ).wait_recv()
+    mixed = returned[...].astype(jnp.float32).reshape(total, HIGH).astype(jnp.bfloat16)
+    summed = jnp.dot(mixed, wo[...], preferred_element_type=jnp.float32)
+    summed = summed + x_own[...].astype(jnp.float32).reshape(total, width)
+    out_ref[...] = summed.reshape(devices, block, width).astype(jnp.bfloat16)
+    for k in order:
+        first[k].wait_send()
+        second[k].wait_send()
+
+
+def local_fused(devices, x, gain, wq, wk, wv, sharp, wo):
+    local_frames, seq_len, width = x.shape
+    positions = seq_len // devices
+    block = local_frames * positions
+    total = devices * block
+    blocks = x.reshape(local_frames, devices, positions, width)
+    blocks = blocks.transpose(1, 0, 2, 3).reshape(devices, block, width)
+    vmem = pl.BlockSpec(memory_space=pltpu.VMEM)
+    anywhere = pl.BlockSpec(memory_space=pl.ANY)
+    dma = pltpu.SemaphoreType.DMA
+    out = pl.pallas_call(
+        functools.partial(fused, devices, local_frames),
+        out_shape=jax.ShapeDtypeStruct(blocks.shape, jnp.bfloat16),
+        in_specs=[pl.BlockSpec(memory_space=pltpu.SMEM), anywhere, vmem] + [anywhere] * 4,
+        out_specs=vmem,
+        scratch_shapes=[
+            pltpu.VMEM(blocks.shape, jnp.bfloat16),
+            pltpu.VMEM(wq.shape, jnp.bfloat16),
+            pltpu.VMEM(wk.shape, jnp.bfloat16),
+            pltpu.VMEM(wv.shape, jnp.bfloat16),
+            pltpu.VMEM(wo.shape, jnp.bfloat16),
+            pltpu.VMEM(blocks.shape, jnp.bfloat16),
+            pltpu.VMEM((total, HIGH), jnp.bfloat16),
+            pltpu.VMEM((total, HIGH), jnp.bfloat16),
+            pltpu.VMEM((total, HIGH), jnp.bfloat16),
+            pltpu.VMEM((devices, block, HIGH), jnp.bfloat16),
+            pltpu.VMEM((devices, block, HIGH), jnp.bfloat16),
+            dma((5,)),
+            dma((devices,)),
+            dma((devices,)),
+            dma((devices,)),
+            dma((devices,)),
+        ],
+        compiler_params=pltpu.CompilerParams(
+            collective_id=0, has_side_effects=True, vmem_limit_bytes=60 * 2**20
+        ),
+    )(sharp, blocks, gain.reshape(1, width), wq, wk, wv, wo)
+    out = out.reshape(devices, local_frames, positions, width).transpose(1, 0, 2, 3)
+    return out.reshape(x.shape)
+
+
 def solution(mesh):
+    devices = mesh.shape["frame"]
+
+    def body(x, *rest):
+        positions = x.shape[1] // devices
+        if devices % 4 == 0 and positions % 8 == 0:
+            return local_fused(devices, x, *rest)
+        return local(x, *rest)
+
     placed = (P(("clips", "frame"), None, None), P(), P(), P(), P(), P(), P())
     return jax.shard_map(
-        local,
+        body,
         mesh=mesh,
         in_specs=placed,
         out_specs=P(("clips", "frame"), None, None),

time: 72.4 us -> 43.8 us (0.60)
  Pallas kernels: 0 us -> 40.2 us
  local copies, waits for them, and re-layouts: 19 us -> 3.26 us
  blocking collectives: 15.3 us -> 0 us
  matrix products: 12.5 us -> 0 us
  other arithmetic: 10.3 us -> 0 us
  starting transfers between devices: 7.51 us -> 0 us
  waiting for transfers between devices: 7.12 us -> 0 us
    pallas_call x0 -> x1, Pallas kernels: none -> 40.2 us  [local_fused(): pl.pallas_call(functools.partial(fused, devices, local_frames), out_shape...]
    all_to_all x1 -> x0, blocking collectives: 15.3 us -> none  [local(): lax.all_to_all(result, 'frame', split_axis=0, concat_axis=1, tiled=True)]
    unnamed x20 -> x1, local copies, waits for them, and re-layouts: 16.4 us -> 1.97 us
    dot_general x6 -> x0, matrix products: 12.5 us -> none  [the longest x1 3.52 us: project_through(): jnp.dot(flat_rows, asking_projection_tensor, preferred_element_type=jnp.f...]
    all_to_all x1 -> x0, starting transfers between devices: 7.51 us -> none  [local(): lax.all_to_all(rescaled_token_vectors, 'frame', split_axis=1, concat_axis...]
    all_to_all x1 -> x0, waiting for transfers between devices: 7.12 us -> none  [local(): lax.all_to_all(rescaled_token_vectors, 'frame', split_axis=1, concat_axis...]
    unnamed x1 -> x0, other arithmetic: 5.49 us -> none
    convert_element_type x2 -> x0, other arithmetic: 1.56 us -> none  [the longest x1 1.31 us: local(): rescaled_token_vectors = (quadratic_average_rescaling(floated) * entry_re...]
  transfers between devices with their start and end apart: 1 -> 0, of which waited for: 1 -> 0; matrix products, arithmetic and copies ran while one was open for 15% -> 0% of each run, Pallas kernels for 0% -> 0%
where the time goes in v1:
time: 43.8 us; the launch traced here: 43.5 us
  Pallas kernels  40.2 us (92%)
  local copies, waits for them, and re-layouts  3.26 us (7%)
    pallas_call x1, Pallas kernels, local_fused(): pl.pallas_call(functools.partial(fused, devices, local_frames), out_shape...  40.2 us
    unnamed x1, local copies, waits for them, and re-layouts  1.97 us
    reshape x1, local copies, waits for them, and re-layouts, local_fused(): gain.reshape(1, width)  1.29 us

profile of v1, /device:TPU:0, one launch (start us, length us, event | category | flops | bytes accessed | tf_op | source)
XLA Modules:
  0.0 43.5 jit_solution(1655520584499964151)
XLA Ops:
  0.0 1.3 %reshape.3.gain_ref = f32[1,1280]{1,0:T(1,128)} reshape(f32[1280]{0:T(1024)} %param.8) | data formatting | bytes 10240 | tf_op jit(solution)/shard_map/reshape | solution.py:298
  1.3 40.2 %shard_map.73 = bf16[32,8,1280]{2,1,0:T(8,128)(2,1)} custom-call(f32[5]{0:T(128)} %sharp_ref.1, bf16[32,8,1280]{2,1,0:T(8,128)(2,1)} %bitcast.3, f32[1,1280]{1,0:T(1,128)} %reshape.3.gain_ref, bf16[1280,640]{1,0:T(8,128)(2,1)} %wq_hbm.1, bf16[1280,640]{1,0:T(8,128)(2,1)} %wk_hbm.1, bf16[1280,640]{1,0:T(8,128)(2,1)} %wv_hbm.1, bf16[640,1280]{1,0:T(8,128)(2,1)} %wo_hbm.1), custom_call_target="tpu_custom_call" | custom-call | tf_op jit(solution)/shard_map/pallas_call | solution.py:272
  41.5 2.0 %copy.9 = bf16[1,256,1280]{2,1,0:T(8,128)(2,1)} copy(bf16[1,256,1280]{2,1,0:T(8,128)(2,1)} %bitcast.2) | data formatting | bytes 1310720

commit v2 on v1

--- a/solution.py
+++ b/solution.py
@@ -114,8 +114,17 @@
 HIGH = HEADS_WIN * CHANNELS_PER_ATT
 
 
-def visiting_order(devices):
-    return sorted(range(1, devices), key=lambda k: (abs(k - devices // 2), k))
+def visiting_order(pairs):
+    return sorted(range(1, pairs), key=lambda k: (-abs(k - pairs // 2), k))
+
+
+def runs(slots):
+    found, first = [], 0
+    for i in range(1, len(slots) + 1):
+        if i == len(slots) or slots[i] != slots[i - 1] + 1:
+            found.append((first, i, slots[first]))
+            first = i
+    return found
 
 
 def fused(
@@ -149,10 +158,13 @@
     me = lax.axis_index("frame")
     block, width = x_own.shape[1], x_own.shape[2]
     positions = block // local_frames
-    order = visiting_order(devices)
+    pairs = devices // 2
+    pair, side = me // 2, lax.rem(me, 2)
+    partner = me + 1 - 2 * side
+    order = visiting_order(pairs)
 
     barrier = pltpu.get_barrier_semaphore()
-    for k in order:
+    for k in range(1, devices):
         pl.semaphore_signal(
             barrier, inc=1, device_id={"frame": lax.rem(me + k, devices)}, device_id_type=MESH
         )
@@ -167,51 +179,79 @@
     loads[0].wait()
     pl.semaphore_wait(barrier, devices - 1)
 
-    first = {}
-    for k in order:
-        target = lax.rem(me + k, devices)
-        first[k] = pltpu.make_async_remote_copy(
+    def send_tokens(target, slot_here, slot_there):
+        copy = pltpu.make_async_remote_copy(
             src_ref=x_own.at[target],
-            dst_ref=gathered.at[k],
-            send_sem=send_a.at[k],
-            recv_sem=recv_a.at[k],
+            dst_ref=gathered.at[slot_there],
+            send_sem=send_a.at[slot_here],
+            recv_sem=recv_a.at[slot_there],
             device_id={"frame": target},
             device_id_type=MESH,
         )
-        first[k].start()
-    gathered[0] = x_own[me]
+        copy.start()
+        return copy
+
+    def token_arrival(slot):
+        return pltpu.make_async_remote_copy(
+            src_ref=x_own.at[0],
+            dst_ref=gathered.at[slot],
+            send_sem=send_a.at[slot],
+            recv_sem=recv_a.at[slot],
+            device_id={"frame": partner},
+            device_id_type=MESH,
+        )
+
+    sent = [send_tokens(partner, 0, side * pairs)]
+    for s in range(2):
+        for k in order:
+            target = lax.rem(pair + k, pairs) * 2 + s
+            sent.append(send_tokens(target, s * pairs + k, side * pairs + k))
+    gathered[side * pairs] = x_own[me]
     for load in loads[1:]:
         load.wait()
 
-    def project(start, stop):
-        rows = (stop - start) * block
-        at = slice(start * block, stop * block)
-        x = gathered[start:stop].astype(jnp.float32).reshape(rows, width)
-        normed = (quadratic_average_rescaling(x) * gain_ref[...]).astype(jnp.bfloat16)
+    def project(slots):
+        parts = [gathered[slot].astype(jnp.float32) for slot in slots]
+        x = jnp.concatenate(parts, axis=0)
+        normed = (quadratic_average_rescaling(x) * gain_ref[...].reshape(1, width)).astype(
+            jnp.bfloat16
+        )
         q = jnp.dot(normed, wq[...], preferred_element_type=jnp.float32)
         k = jnp.dot(normed, wk[...], preferred_element_type=jnp.float32)
         v = jnp.dot(normed, wv[...], preferred_element_type=jnp.float32)
         for h in range(HEADS_WIN):
             c = slice(h * CHANNELS_PER_ATT, (h + 1) * CHANNELS_PER_ATT)
-            q_rows[at, c] = (
+            qs = (
                 quadratic_average_rescaling(q[:, c]) * sharp_ref[h] / math.sqrt(CHANNELS_PER_ATT)
             ).astype(jnp.bfloat16)
-            k_rows[at, c] = quadratic_average_rescaling(k[:, c]).astype(jnp.bfloat16)
-        v_rows[at, :] = v.astype(jnp.bfloat16)
-
-    quarter = devices // 4
-    pieces = ((quarter, devices - quarter), (devices - quarter, devices), (0, quarter))
-    for start, stop in pieces:
-        for k in range(max(start, 1), stop):
-            first[k].wait_recv()
-        project(start, stop)
+            ks = quadratic_average_rescaling(k[:, c]).astype(jnp.bfloat16)
+            vs = v[:, c].astype(jnp.bfloat16)
+            for first, last, to in runs(slots):
+                a = slice(first * block, last * block)
+                b = slice(to * block, (to + last - first) * block)
+                q_rows[b, c] = qs[a]
+                k_rows[b, c] = ks[a]
+                v_rows[b, c] = vs[a]
+
+    half = pairs // 2
+    early, late = [0] + order[: half - 1], order[half - 1 :]
+    for piece in (early, late):
+        for s in range(2):
+            for k in piece:
+                if k:
+                    token_arrival(s * pairs + k).wait_recv()
+        if 0 in piece:
+            token_arrival((1 - side) * pairs).wait_recv()
+        project(sorted(s * pairs + k for s in range(2) for k in piece))
 
     total = devices * block
     def ids(axis):
         r = lax.broadcasted_iota(jnp.int32, (total, total), axis)
         slot = r // block
-        owner = me - slot
-        owner = jnp.where(owner < 0, owner + devices, owner)
+        slot_side = slot // pairs
+        source = pair - (slot - slot_side * pairs)
+        source = jnp.where(source < 0, source + pairs, source)
+        owner = source * 2 + slot_side
         inner = r - slot * block
         return owner * local_frames + inner // positions, inner % positions
 
@@ -228,35 +268,48 @@
         attended = jnp.dot(weights, v_rows[:, c], preferred_element_type=jnp.float32)
         outgoing[:, :, c] = attended.reshape(devices, block, CHANNELS_PER_ATT).astype(jnp.bfloat16)
 
-    second = {}
-    for k in order:
-        target = lax.rem(me + devices - k, devices)
-        second[k] = pltpu.make_async_remote_copy(
-            src_ref=outgoing.at[k],
-            dst_ref=returned.at[me],
-            send_sem=send_b.at[k],
-            recv_sem=recv_b.at[k],
+    def send_back(target, slot_here, slot_there):
+        copy = pltpu.make_async_remote_copy(
+            src_ref=outgoing.at[slot_here],
+            dst_ref=returned.at[side, pair],
+            send_sem=send_b.at[slot_here],
+            recv_sem=recv_b.at[slot_there],
             device_id={"frame": target},
             device_id_type=MESH,
         )
-        second[k].start()
-    returned[me] = outgoing[0]
+        copy.start()
+        return copy
+
+    def arrival(s, k):
+        return pltpu.make_async_remote_copy(
+            src_ref=outgoing.at[0],
+            dst_ref=returned.at[s, lax.rem(pair + k, pairs)],
+            send_sem=send_b.at[0],
+            recv_sem=recv_b.at[s * pairs + k],
+            device_id={"frame": partner},
+            device_id_type=MESH,
+        )
+
     for k in order:
-        pltpu.make_async_remote_copy(
-            src_ref=outgoing.at[k],
-            dst_ref=returned.at[lax.rem(me + k, devices)],
-            send_sem=send_b.at[k],
-            recv_sem=recv_b.at[k],
-            device_id={"frame": lax.rem(me + devices - k, devices)},
-            device_id_type=MESH,
-        ).wait_recv()
-    mixed = returned[...].astype(jnp.float32).reshape(total, HIGH).astype(jnp.bfloat16)
-    summed = jnp.dot(mixed, wo[...], preferred_element_type=jnp.float32)
-    summed = summed + x_own[...].astype(jnp.float32).reshape(total, width)
-    out_ref[...] = summed.reshape(devices, block, width).astype(jnp.bfloat16)
-    for k in order:
-        first[k].wait_send()
-        second[k].wait_send()
+        for s in range(2):
+            target = lax.rem(pair + pairs - k, pairs) * 2 + s
+            sent.append(send_back(target, s * pairs + k, side * pairs + k))
+    sent.append(send_back(partner, (1 - side) * pairs, side * pairs))
+    returned[side, pair] = outgoing[side * pairs]
+    arrival(1 - side, 0).wait_recv()
+    for s in range(2):
+        for k in order:
+            arrival(s, k).wait_recv()
+        rows = pairs * block
+        mixed = returned[s].astype(jnp.float32).reshape(rows, HIGH).astype(jnp.bfloat16)
+        summed = jnp.dot(mixed, wo[...], preferred_element_type=jnp.float32)
+        for k in range(pairs):
+            j = 2 * k + s
+            out_ref[j] = (
+                summed[k * block : (k + 1) * block] + x_own[j].astype(jnp.float32)
+            ).astype(jnp.bfloat16)
+    for copy in sent:
+        copy.wait_send()
 
 
 def local_fused(devices, x, gain, wq, wk, wv, sharp, wo):
@@ -271,7 +324,7 @@
     dma = pltpu.SemaphoreType.DMA
     out = pl.pallas_call(
         functools.partial(fused, devices, local_frames),
-        out_shape=jax.ShapeDtypeStruct(blocks.shape, jnp.bfloat16),
+        out_shape=pltpu.VMEM(blocks.shape, jnp.bfloat16),
         in_specs=[pl.BlockSpec(memory_space=pltpu.SMEM), anywhere, vmem] + [anywhere] * 4,
         out_specs=vmem,
         scratch_shapes=[
@@ -285,7 +338,7 @@
             pltpu.VMEM((total, HIGH), jnp.bfloat16),
             pltpu.VMEM((total, HIGH), jnp.bfloat16),
             pltpu.VMEM((devices, block, HIGH), jnp.bfloat16),
-            pltpu.VMEM((devices, block, HIGH), jnp.bfloat16),
+            pltpu.VMEM((2, devices // 2, block, HIGH), jnp.bfloat16),
             dma((5,)),
             dma((devices,)),
             dma((devices,)),
@@ -295,7 +348,7 @@
         compiler_params=pltpu.CompilerParams(
             collective_id=0, has_side_effects=True, vmem_limit_bytes=60 * 2**20
         ),
-    )(sharp, blocks, gain.reshape(1, width), wq, wk, wv, wo)
+    )(sharp, blocks, gain, wq, wk, wv, wo)
     out = out.reshape(devices, local_frames, positions, width).transpose(1, 0, 2, 3)
     return out.reshape(x.shape)
 

time: 43.8 us -> 32.8 us (0.75)
  Pallas kernels: 40.2 us -> 31.8 us
  local copies, waits for them, and re-layouts: 3.26 us -> 0.84 us
    pallas_call x1, Pallas kernels: 40.2 us -> 31.8 us  [local_fused(): pl.pallas_call(functools.partial(fused, devices, local_frames), out_shape...]
    reshape x1 -> x0, local copies, waits for them, and re-layouts: 1.29 us -> none  [local_fused(): gain.reshape(1, width)]
    unnamed x1, local copies, waits for them, and re-layouts: 1.97 us -> 0.84 us
where the time goes in v2:
time: 32.8 us; the launch traced here: 32.6 us
  Pallas kernels  31.8 us (97%)
  local copies, waits for them, and re-layouts  0.84 us (3%)
    pallas_call x1, Pallas kernels, local_fused(): pl.pallas_call(functools.partial(fused, devices, local_frames), out_shape...  31.8 us
    unnamed x1, local copies, waits for them, and re-layouts  0.84 us

profile of v2, /device:TPU:0, one launch (start us, length us, event | category | flops | bytes accessed | tf_op | source)
XLA Modules:
  0.0 32.6 jit_solution(13046863826810476393)
XLA Ops:
  0.0 31.8 %shard_map.73 = bf16[32,8,1280]{2,1,0:T(8,128)(2,1)S(1)} custom-call(f32[5]{0:T(128)} %sharp_ref.1, bf16[32,8,1280]{2,1,0:T(8,128)(2,1)} %bitcast.3, f32[1280]{0:T(1024)} %gain_ref.1, bf16[1280,640]{1,0:T(8,128)(2,1)} %wq_hbm.1, bf16[1280,640]{1,0:T(8,128)(2,1)} %wk_hbm.1, bf16[1280,640]{1,0:T(8,128)(2,1)} %wv_hbm.1, bf16[640,1280]{1,0:T(8,128)(2,1)} %wo_hbm.1), custom_call_target="tpu_custom_call" | custom-call | tf_op jit(solution)/shard_map/pallas_call | solution.py:325
  31.8 0.8 %copy.9 = bf16[1,256,1280]{2,1,0:T(8,128)(2,1)} copy(bf16[1,256,1280]{2,1,0:T(8,128)(2,1)S(1)} %bitcast.2) | data formatting | bytes 1310720

commit v3 on v2

--- a/solution.py
+++ b/solution.py
@@ -233,6 +233,23 @@
                 k_rows[b, c] = ks[a]
                 v_rows[b, c] = vs[a]
 
+    total = devices * block
+
+    def ids(axis):
+        shape = (total, 1) if axis == 0 else (1, total)
+        r = lax.broadcasted_iota(jnp.int32, shape, axis)
+        slot = r // block
+        slot_side = slot // pairs
+        source = pair - (slot - slot_side * pairs)
+        source = jnp.where(source < 0, source + pairs, source)
+        owner = source * 2 + slot_side
+        inner = r - slot * block
+        return owner * local_frames + inner // positions, inner % positions
+
+    t_row, p_row = ids(0)
+    t_col, p_col = ids(1)
+    offset = t_row - t_col
+    inside = (p_row == p_col) & (offset >= 0) & (offset < WINDOW)
     half = pairs // 2
     early, late = [0] + order[: half - 1], order[half - 1 :]
     for piece in (early, late):
@@ -244,21 +261,6 @@
             token_arrival((1 - side) * pairs).wait_recv()
         project(sorted(s * pairs + k for s in range(2) for k in piece))
 
-    total = devices * block
-    def ids(axis):
-        r = lax.broadcasted_iota(jnp.int32, (total, total), axis)
-        slot = r // block
-        slot_side = slot // pairs
-        source = pair - (slot - slot_side * pairs)
-        source = jnp.where(source < 0, source + pairs, source)
-        owner = source * 2 + slot_side
-        inner = r - slot * block
-        return owner * local_frames + inner // positions, inner % positions
-
-    t_row, p_row = ids(0)
-    t_col, p_col = ids(1)
-    offset = t_row - t_col
-    inside = (p_row == p_col) & (offset >= 0) & (offset < WINDOW)
     for h in range(HEADS_WIN):
         c = slice(h * CHANNELS_PER_ATT, (h + 1) * CHANNELS_PER_ATT)
         scores = lax.dot_general(

time: 32.8 us -> 32.7 us (level)
  no operation moved by 1% of the time
where the time goes in v3:
time: 32.7 us; the launch traced here: 32.5 us
  Pallas kernels  31.7 us (97%)
  local copies, waits for them, and re-layouts  0.84 us (3%)
    pallas_call x1, Pallas kernels, local_fused(): pl.pallas_call(functools.partial(fused, devices, local_frames), out_shape...  31.7 us
    unnamed x1, local copies, waits for them, and re-layouts  0.84 us

profile of v3, /device:TPU:0, one launch (start us, length us, event | category | flops | bytes accessed | tf_op | source)
XLA Modules:
  0.0 32.5 jit_solution(16160747394424191876)
XLA Ops:
  0.0 31.7 %shard_map.73 = bf16[32,8,1280]{2,1,0:T(8,128)(2,1)S(1)} custom-call(f32[5]{0:T(128)} %sharp_ref.1, bf16[32,8,1280]{2,1,0:T(8,128)(2,1)} %bitcast.3, f32[1280]{0:T(1024)} %gain_ref.1, bf16[1280,640]{1,0:T(8,128)(2,1)} %wq_hbm.1, bf16[1280,640]{1,0:T(8,128)(2,1)} %wk_hbm.1, bf16[1280,640]{1,0:T(8,128)(2,1)} %wv_hbm.1, bf16[640,1280]{1,0:T(8,128)(2,1)} %wo_hbm.1), custom_call_target="tpu_custom_call" | custom-call | tf_op jit(solution)/shard_map/pallas_call | solution.py:327
  31.7 0.8 %copy.9 = bf16[1,256,1280]{2,1,0:T(8,128)(2,1)} copy(bf16[1,256,1280]{2,1,0:T(8,128)(2,1)S(1)} %bitcast.2) | data formatting | bytes 1310720
